TPU v7x, 32 devices: a whole 2x2x4 slice. The times are simulated.
32 devices in a mesh: lon: 8 (over y, x, core), lat: 4 (over z).
Axes of the slice: x: 2, y: 2, z: 4, core: 2. Of those that a mesh axis runs over, the one named last changes fastest.
Arguments:
- fields: bfloat16 [32, 256, 256], P('lat', 'lon'), may hold values from -6 to 6
- norm_lon: float32 [256], replicated, may hold values from 0.25 to 1.75
- query_lon: bfloat16 [256, 256], replicated, may hold values from -0.375 to 0.375
- key_lon: bfloat16 [256, 256], replicated, may hold values from -0.375 to 0.375
- value_lon: bfloat16 [256, 256], replicated, may hold values from -0.375 to 0.375
- out_lon: bfloat16 [256, 256], replicated, may hold values from -0.375 to 0.375
- temp_lon: float32 [8], replicated, may hold values from 0.5 to 12
- bias_lon: float32 [8], replicated, may hold values from -2 to 2
- norm_lat: float32 [256], replicated, may hold values from 0.25 to 1.75
- query_lat: bfloat16 [256, 256], replicated, may hold values from -0.375 to 0.375
- key_lat: bfloat16 [256, 256], replicated, may hold values from -0.375 to 0.375
- value_lat: bfloat16 [256, 256], replicated, may hold values from -0.375 to 0.375
- out_lat: bfloat16 [256, 256], replicated, may hold values from -0.375 to 0.375
- temp_lat: float32 [8], replicated, may hold values from 0.5 to 12
- bias_lat: float32 [8], replicated, may hold values from -4 to 0
- norm_mlp: float32 [256], replicated, may hold values from 0.25 to 1.75
- w_gate: bfloat16 [256, 1024], replicated, may hold values from -0.375 to 0.375
- w_up: bfloat16 [256, 1024], replicated, may hold values from -0.375 to 0.375
- w_down: bfloat16 [1024, 256], replicated, may hold values from -0.1875 to 0.1875
Outputs:
- updated: bfloat16 [32, 256, 256], P('lat', 'lon')
All inputs are finite; a program needn't handle non-finite values.
Results may differ from a plain program's by a relative error of at most 0.018.
The roundings to bfloat16 on the way count: a program that leaves them out, or rounds other values in their place, can miss the bound.
Values may be sent and summed in bfloat16 or wider, within the bound.
A program may use at most 64 MiB of HBM per device.

v0:
```python
import math
import jax
import jax.numpy as jnp
from jax import lax
from jax.sharding import PartitionSpec as P


def normalize(values, gain):
    factor = lax.rsqrt(jnp.mean(values * values, axis=-1, keepdims=True) + 1e-06)
    return (values * factor * gain).astype(jnp.bfloat16)


def project(values, weight):
    return jnp.dot(values, weight, preferred_element_type=jnp.float32).astype(jnp.bfloat16)


def attend_lat(queries, keys, values, temp, bias):
    count, cols, depth = queries.shape
    heads = temp.shape[0]
    size = depth // heads
    qh = queries.reshape(count, cols, heads, size)
    kh = keys.reshape(count, cols, heads, size)
    vh = values.reshape(count, cols, heads, size)
    scores = jnp.einsum("ichd,jchd->chij", qh, kh, preferred_element_type=jnp.float32)
    place = jnp.arange(count, dtype=jnp.int32)
    spread = jnp.abs(place[:, None] - place[None, :]).astype(jnp.float32) / count
    scores = (
        scores * (temp / math.sqrt(size))[None, :, None, None]
        + bias[None, :, None, None] * spread[None, None]
    )
    expo = jnp.exp(scores - jnp.max(scores, axis=-1, keepdims=True))
    denom = jnp.sum(expo, axis=-1)
    mixed = jnp.einsum(
        "chij,jchd->ichd", expo.astype(jnp.bfloat16), vh, preferred_element_type=jnp.float32
    )
    mixed = mixed / jnp.transpose(denom, (2, 0, 1))[..., None]
    return mixed.astype(jnp.bfloat16).reshape(count, cols, depth)


def body(
    fields,
    norm_lon,
    query_lon,
    key_lon,
    value_lon,
    out_lon,
    temp_lon,
    bias_lon,
    norm_lat,
    query_lat,
    key_lat,
    value_lat,
    out_lat,
    temp_lat,
    bias_lat,
    norm_mlp,
    w_gate,
    w_up,
    w_down,
):
    rows, width, depth = fields.shape
    heads = temp_lon.shape[0]
    size = depth // heads
    total_lon = width * lax.axis_size("lon")
    resid = fields.astype(jnp.float32)
    normed = normalize(resid, norm_lon)
    scale_lon = temp_lon / math.sqrt(size)
    query_place = lax.axis_index("lon") * width + jnp.arange(width, dtype=jnp.int32)
    queries = project(normed, query_lon).reshape(rows, width, heads, size)
    piece = lax.all_gather(normed, "lon", axis=1, tiled=True)
    keys = project(piece, key_lon)
    count = keys.shape[1]
    key_place = jnp.arange(count, dtype=jnp.int32)
    angle = (query_place[:, None] - key_place[None, :]).astype(jnp.float32) * (
        2.0 * math.pi / total_lon
    )
    wave = jnp.cos(angle)

    def one_row(items):
        query_row, key_row, value_row, peak, total, accum = items
        key_heads = key_row.reshape(count, heads, size)
        value_heads = value_row.reshape(count, heads, size)
        scores = jnp.einsum(
            "ihd,jhd->hij", query_row, key_heads, preferred_element_type=jnp.float32
        )
        scores = scores * scale_lon[:, None, None] + bias_lon[:, None, None] * wave[None]
        fresh = jnp.maximum(peak, jnp.max(scores, axis=-1))
        shrink = jnp.exp(peak - fresh)
        expo = jnp.exp(scores - fresh[..., None])
        total = total * shrink + jnp.sum(expo, axis=-1)
        mixed = jnp.einsum(
            "hij,jhd->ihd",
            expo.astype(jnp.bfloat16),
            value_heads,
            preferred_element_type=jnp.float32,
        )
        accum = accum.reshape(width, heads, size) * jnp.transpose(shrink)[:, :, None] + mixed
        return (fresh, total, accum.reshape(width, depth))

    peak = jnp.full((rows, heads, width), -1e30, jnp.float32)
    total = jnp.zeros((rows, heads, width), jnp.float32)
    accum = jnp.zeros((rows, width, depth), jnp.float32)
    peak, total, accum = lax.map(
        one_row, (queries, keys, project(piece, value_lon), peak, total, accum)
    )
    attended = accum.reshape(rows, width, heads, size) / jnp.transpose(total, (0, 2, 1))[..., None]
    attended = attended.astype(jnp.bfloat16).reshape(rows, width, depth)
    first = resid + jnp.dot(attended, out_lon, preferred_element_type=jnp.float32)
    normed_lat = normalize(first, norm_lat)
    query_col = project(normed_lat, query_lat)
    key_col = project(normed_lat, key_lat)
    value_col = project(normed_lat, value_lat)
    query_col, key_col, value_col = (
        lax.all_to_all(query_col, "lat", split_axis=1, concat_axis=0, tiled=True),
        lax.all_to_all(key_col, "lat", split_axis=1, concat_axis=0, tiled=True),
        lax.all_to_all(value_col, "lat", split_axis=1, concat_axis=0, tiled=True),
    )
    mixed_lat = attend_lat(query_col, key_col, value_col, temp_lat, bias_lat)
    returned = lax.all_to_all(mixed_lat, "lat", split_axis=0, concat_axis=1, tiled=True)
    second = first + jnp.dot(returned, out_lat, preferred_element_type=jnp.float32)
    normed_mlp = normalize(second, norm_mlp)
    gate = jnp.dot(normed_mlp, w_gate, preferred_element_type=jnp.float32)
    upper = jnp.dot(normed_mlp, w_up, preferred_element_type=jnp.float32)
    hidden = (jax.nn.silu(gate) * upper).astype(jnp.bfloat16)
    return (second + jnp.dot(hidden, w_down, preferred_element_type=jnp.float32)).astype(
        jnp.bfloat16
    )


def solution(mesh):
    in_specs = (
        P("lat", "lon", None),
        P(),
        P(),
        P(),
        P(),
        P(),
        P(),
        P(),
        P(),
        P(),
        P(),
        P(),
        P(),
        P(),
        P(),
        P(),
        P(),
        P(),
        P(),
    )
    out_specs = P("lat", "lon", None)
    return jax.shard_map(body, mesh=mesh, in_specs=in_specs, out_specs=out_specs, check_vma=False)
```

profile of v0, /device:TPU:0, one launch (start us, length us, event | category | flops | bytes accessed | tf_op | source)
XLA Modules:
  0.0 112.4 jit_solution(1554158160764497591)
XLA Ops:
  6.6 1.1 fusion.35
  7.7 1.7 %fusion.37 = bf16[8,32,256]{2,1,0:T(8,128)(2,1)} fusion(bf16[8,32,256]{2,1,0:T(8,128)(2,1)} %param.21, f32[256]{0:T(256)} %param.22, f32[8,32]{1,0:T(8,128)S(1)} %add_rsqrt_fusion.2), kind=kLoop, calls=%fused_computation.60 | loop fusion | flops 262144 | bytes 264192 | tf_op jit(solution)/shard_map/convert_element_type | solution.py:10
  9.4 1.2 %convolution_convert_fusion.5 = bf16[8,32,256]{2,1,0:T(8,128)(2,1)S(1)} fusion(bf16[8,32,256]{2,1,0:T(8,128)(2,1)} %fusion.37, bf16[256,256]{1,0:T(8,128)(2,1)} %param.23), kind=kOutput, calls=%fused_computation.36 | convolution fusion | flops 33619968 | bytes 393216 | tf_op jit(solution)/shard_map/dot_general | solution.py:14
  10.6 1.0 reshape.126
  11.7 23.9 %all-gather.2.cloned.1.call-done = bf16[8,256,256]{2,1,0:T(8,128)(2,1)} async-done(((bf16[8,32,256]{2,1,0:T(8,128)(2,1)}), bf16[8,256,256]{2,1,0:T(8,128)(2,1)}) %all-gather.2.cloned.1.call-update) | async-done | bytes 1048592 | tf_op jit(solution)/shard_map/all_gather | solution.py:70
  35.6 1.7 %convolution_convert_fusion.1 = bf16[8,256,256]{2,1,0:T(8,128)(2,1)S(1)} fusion(bf16[8,256,256]{2,1,0:T(8,128)(2,1)} %all-gather.2.cloned.1.call-done, bf16[256,256]{1,0:T(8,128)(2,1)S(1)} %copy-done.3), kind=kOutput, calls=%fused_computation.20 | convolution fusion | flops 268959744 | bytes 2228224 | tf_op jit(solution)/shard_map/dot_general | solution.py:14
  37.4 0.4 convolution_convert_fusion
  38.1 21.5 %while.13 = (s32[]{:T(128)}, f32[8,8,32]{2,1,0:T(8,128)S(1)}, f32[8,32,256]{1,2,0:T(8,128)}, bf16[8,32,8,32]{3,2,1,0:T(8,128)(2,1)}, bf16[8,256,256]{2,1,0:T(8,1...) while((s32[]{:T(128)}, f32[8,8,32]{2,1,0:T(8,128)S(1)}, ...), condition=%wide.region_4.5_spmd.clone, body=%wide.region_1.4_spmd.clone.sunk | while | flops 8946946 | bytes 2429245 | solution.py:103
  38.4 0.9 constant_dynamic-slice_fusion.6
  39.8 0.2 fusion.79
  40.1 0.7 constant_dynamic-update-slice_fusion.2
  41.1 0.9 constant_dynamic-slice_fusion.6
  42.5 0.2 fusion.79
  42.8 0.7 constant_dynamic-update-slice_fusion.2
  43.8 0.9 constant_dynamic-slice_fusion.6
  45.2 0.2 fusion.79
  45.5 0.7 constant_dynamic-update-slice_fusion.2
  46.5 0.9 constant_dynamic-slice_fusion.6
  47.9 0.2 fusion.79
  48.1 0.7 constant_dynamic-update-slice_fusion.2
  49.1 0.9 constant_dynamic-slice_fusion.6
  50.8 0.7 constant_dynamic-update-slice_fusion.2
  51.8 0.9 constant_dynamic-slice_fusion.6
  53.5 0.7 constant_dynamic-update-slice_fusion.2
  54.5 0.9 constant_dynamic-slice_fusion.6
  56.2 0.7 constant_dynamic-update-slice_fusion.2
  57.2 0.9 constant_dynamic-slice_fusion.6
  58.9 0.7 constant_dynamic-update-slice_fusion.2
  59.5 1.4 %fusion.16 = bf16[8,32,256]{1,2,0:T(8,128)(2,1)S(1)} fusion(f32[8,32,256]{1,2,0:T(8,128)} %get-tuple-element.53, f32[8,32,8]{1,2,0:T(8,128)S(1)} %bitcast.131), kind=kLoop, calls=%fused_computation.38 | loop fusion | flops 131072 | bytes 401408 | tf_op jit(solution)/shard_map/convert_element_type | solution.py:107
  61.0 0.4 multiply_reduce_fusion.1
  61.5 0.3 copy-done.5
  62.0 0.7 copy.48
  62.8 4.7 %all-to-all-start.2 = ((bf16[8,32,256]{2,0,1:T(8,128)(2,1)}), bf16[8,32,256]{2,0,1:T(8,128)(2,1)S(1)}, u32[]{:S(2)}, u32[]{:S(2)}) async-start(bf16[8,32,256]{2,0,1:T(8,128)(2,1)} %copy.48), calls=%async_computation.2 | async-start | bytes 262144 | tf_op jit(solution)/shard_map/all_to_all | solution.py:115
  67.7 0.7 copy.46
  68.4 5.4 %all-to-all-done.2 = bf16[8,32,256]{2,0,1:T(8,128)(2,1)S(1)} async-done(((bf16[8,32,256]{2,0,1:T(8,128)(2,1)}), bf16[8,32,256]{2,0,1:T(8,128)(2,1)S(1)}, u32[]{:S(2)}, u32[]{:S(2)}) %all-to-all-start.2) | async-done | bytes 131104 | tf_op jit(solution)/shard_map/all_to_all | solution.py:115
  73.8 3.3 %all-to-all-start.1 = ((bf16[8,32,256]{2,0,1:T(8,128)(2,1)}), bf16[8,32,256]{2,0,1:T(8,128)(2,1)S(1)}, u32[]{:S(2)}, u32[]{:S(2)}) async-start(bf16[8,32,256]{2,0,1:T(8,128)(2,1)} %copy.46), calls=%async_computation.1 | async-start | bytes 262144 | tf_op jit(solution)/shard_map/all_to_all | solution.py:114
  77.3 0.7 copy.44
  78.0 5.0 %all-to-all-done.1 = bf16[8,32,256]{2,0,1:T(8,128)(2,1)S(1)} async-done(((bf16[8,32,256]{2,0,1:T(8,128)(2,1)}), bf16[8,32,256]{2,0,1:T(8,128)(2,1)S(1)}, u32[]{:S(2)}, u32[]{:S(2)}) %all-to-all-start.1) | async-done | bytes 131104 | tf_op jit(solution)/shard_map/all_to_all | solution.py:114
  83.0 3.3 %all-to-all-start = ((bf16[8,32,256]{2,0,1:T(8,128)(2,1)}), bf16[8,32,256]{2,0,1:T(8,128)(2,1)S(1)}, u32[]{:S(2)}, u32[]{:S(2)}) async-start(bf16[8,32,256]{2,0,1:T(8,128)(2,1)} %copy.44), calls=%async_computation | async-start | bytes 262144 | tf_op jit(solution)/shard_map/all_to_all | solution.py:116
  86.9 5.3 %all-to-all-done = bf16[8,32,256]{2,0,1:T(8,128)(2,1)S(1)} async-done(((bf16[8,32,256]{2,0,1:T(8,128)(2,1)}), bf16[8,32,256]{2,0,1:T(8,128)(2,1)S(1)}, u32[]{:S(2)}, u32[]{:S(2)}) %all-to-all-start) | async-done | bytes 131104 | tf_op jit(solution)/shard_map/all_to_all | solution.py:116
  92.5 0.9 fusion.56
  93.4 0.3 fusion.22
  93.7 0.6 fusion.11
  94.5 8.4 %all_to_all.63 = bf16[32,8,256]{2,1,0:T(8,128)(2,1)S(1)} all-to-all(bf16[32,8,256]{2,1,0:T(8,128)(2,1)S(1)} %copy.54), channel_id=1, replica_groups=mesh['lon'=8,'lat'=4] {'lat'}, dimensions={0} | all-to-all | bytes 262144 | tf_op jit(solution)/shard_map/all_to_all | solution.py:119
  102.9 0.3 multiply_reduce_fusion
  103.2 0.3 fusion.28
  103.5 0.6 copy-done.14
  104.4 1.2 %fusion.15 = bf16[8,32,256]{2,1,0:T(8,128)(2,1)} fusion(f32[8,32,256]{2,1,0:T(8,128)S(1)} %get-tuple-element.132, f32[8,32,1024]{2,1,0:T(8,128)S(1)} %fusion.28, bf16[1024,256]{1,0:T(8,128)(2,1)S(1)} %copy-done.14, bf16[256,1024]{1,0:T(8,128)(2,1)S(1)} %copy-done.15, f32[256]{0:T(256)S(1)} %copy-done.12, f32[8,32]{1,0:T(8,128)S(1)} %add_rsqrt_fusion), kind=kOutput, calls=%fused_computation.32 | convolution fusion | flops 270336000 | bytes 2492416 | tf_op jit(solution)/shard_map/dot_general | solution.py:125
  (125 shorter events, 10.2 us)
Async XLA Ops:
  6.5 96.7 %copy-start = (bf16[256,1024]{1,0:T(8,128)(2,1)S(1)}, bf16[256,1024]{1,0:T(8,128)(2,1)}, u32[]{:S(2)}) copy-start(bf16[256,1024]{1,0:T(8,128)(2,1)} %param.37) | copy-start | bytes 1572868
  6.5 5.1 %copy-start.16 = (f32[8]{0:T(128)S(1)}, f32[8]{0:T(128)}, u32[]{:S(2)}) copy-start(f32[8]{0:T(128)} %param.27) | copy-start | bytes 100
  6.5 5.1 %copy-start.13 = (f32[8]{0:T(128)S(1)}, f32[8]{0:T(128)}, u32[]{:S(2)}) copy-start(f32[8]{0:T(128)} %param.35) | copy-start | bytes 100
  6.5 29.1 %copy-start.3 = (bf16[256,256]{1,0:T(8,128)(2,1)S(1)}, bf16[256,256]{1,0:T(8,128)(2,1)}, u32[]{:S(2)}) copy-start(bf16[256,256]{1,0:T(8,128)(2,1)} %param.24) | copy-start | bytes 393220
  6.5 29.1 %all-gather.2.cloned.1.call-start = ((), (), s32[]{:S(2)}) async-start(), calls=%async_computation.4 | async-start | bytes 1179648 | tf_op jit(solution)/shard_map/all_gather | solution.py:70
  11.7 25.7 %copy-start.4 = (bf16[256,256]{1,0:T(8,128)(2,1)S(1)}, bf16[256,256]{1,0:T(8,128)(2,1)}, u32[]{:S(2)}) copy-start(bf16[256,256]{1,0:T(8,128)(2,1)} %param.25) | copy-start | bytes 393220
  35.6 1.8 %copy-start.1 = (bf16[8,256,256]{2,1,0:T(8,128)(2,1)S(1)}, bf16[8,256,256]{2,1,0:T(8,128)(2,1)}, u32[]{:S(2)}) copy-start(bf16[8,256,256]{2,1,0:T(8,128)(2,1)} %all-gather.2.cloned.1.call-done) | copy-start | bytes 3145732
  37.4 0.7 copy-start.10
  59.5 1.4 %copy-start.2 = (bf16[8,32,256]{2,1,0:T(8,128)(2,1)S(1)}, bf16[8,32,256]{2,1,0:T(8,128)(2,1)}, u32[]{:S(2)}) copy-start(bf16[8,32,256]{2,1,0:T(8,128)(2,1)} %param.21) | copy-start | bytes 393220
  59.5 1.4 %copy-start.9 = (bf16[256,256]{1,0:T(8,128)(2,1)S(1)}, bf16[256,256]{1,0:T(8,128)(2,1)}, u32[]{:S(2)}) copy-start(bf16[256,256]{1,0:T(8,128)(2,1)} %param.26) | copy-start | bytes 393220
  59.5 1.8 %copy-start.11 = (f32[256]{0:T(256)S(1)}, f32[256]{0:T(256)}, u32[]{:S(2)}) copy-start(f32[256]{0:T(256)} %param.29) | copy-start | bytes 3076
  60.9 0.9 copy-start.5
  60.9 6.5 %copy-start.6 = (bf16[256,256]{1,0:T(8,128)(2,1)S(1)}, bf16[256,256]{1,0:T(8,128)(2,1)}, u32[]{:S(2)}) copy-start(bf16[256,256]{1,0:T(8,128)(2,1)} %param.30) | copy-start | bytes 393220
  61.4 15.7 %copy-start.7 = (bf16[256,256]{1,0:T(8,128)(2,1)S(1)}, bf16[256,256]{1,0:T(8,128)(2,1)}, u32[]{:S(2)}) copy-start(bf16[256,256]{1,0:T(8,128)(2,1)} %param.32) | copy-start | bytes 393220
  62.8 23.6 %copy-start.17 = (f32[8]{0:T(128)S(1)}, f32[8]{0:T(128)}, u32[]{:S(2)}) copy-start(f32[8]{0:T(128)} %param.34) | copy-start | bytes 100
  62.8 11.0 %all-to-all-start.2 = ((bf16[8,32,256]{2,0,1:T(8,128)(2,1)}), bf16[8,32,256]{2,0,1:T(8,128)(2,1)S(1)}, u32[]{:S(2)}, u32[]{:S(2)}) async-start(bf16[8,32,256]{2,0,1:T(8,128)(2,1)} %copy.48), calls=%async_computation.2 | async-start | bytes 262144 | tf_op jit(solution)/shard_map/all_to_all | solution.py:115
  73.8 9.2 %all-to-all-start.1 = ((bf16[8,32,256]{2,0,1:T(8,128)(2,1)}), bf16[8,32,256]{2,0,1:T(8,128)(2,1)S(1)}, u32[]{:S(2)}, u32[]{:S(2)}) async-start(bf16[8,32,256]{2,0,1:T(8,128)(2,1)} %copy.46), calls=%async_computation.1 | async-start | bytes 262144 | tf_op jit(solution)/shard_map/all_to_all | solution.py:114
  83.0 9.2 %all-to-all-start = ((bf16[8,32,256]{2,0,1:T(8,128)(2,1)}), bf16[8,32,256]{2,0,1:T(8,128)(2,1)S(1)}, u32[]{:S(2)}, u32[]{:S(2)}) async-start(bf16[8,32,256]{2,0,1:T(8,128)(2,1)} %copy.44), calls=%async_computation | async-start | bytes 262144 | tf_op jit(solution)/shard_map/all_to_all | solution.py:116
  93.6 9.2 %copy-start.8 = (bf16[256,256]{1,0:T(8,128)(2,1)S(1)}, bf16[256,256]{1,0:T(8,128)(2,1)}, u32[]{:S(2)}) copy-start(bf16[256,256]{1,0:T(8,128)(2,1)} %param.33) | copy-start | bytes 393220
  94.2 9.0 %copy-start.12 = (f32[256]{0:T(256)S(1)}, f32[256]{0:T(256)}, u32[]{:S(2)}) copy-start(f32[256]{0:T(256)} %param.36) | copy-start | bytes 3076
  103.1 1.0 copy-start.14
  103.2 1.2 %copy-start.15 = (bf16[256,1024]{1,0:T(8,128)(2,1)S(1)}, bf16[256,1024]{1,0:T(8,128)(2,1)}, u32[]{:S(2)}) copy-start(bf16[256,1024]{1,0:T(8,128)(2,1)} %param.38) | copy-start | bytes 1572868
Sparse Core Ops, SparseCore 0:
  9.5 26.0 all-gather.1
where the time goes:
time: 113 us; the launch traced here: 112 us
  waiting for transfers between devices  39.5 us (35%)
  local copies, waits for them, and re-layouts  19.6 us (17%)
  between operations  13.8 us (12%)
  starting transfers between devices  11.4 us (10%)
  matrix products  11.4 us (10%)
  blocking collectives  8.41 us (7%)
  other arithmetic  7.81 us (7%)
    all_gather x1, waiting for transfers between devices, body(): piece = lax.all_gather(normed, 'lon', axis=1, tiled=True)  23.9 us
    dynamic_slice x32, local copies, waits for them, and re-layouts, body(): lax.map(one_row, (queries, keys, project(piece, value_lon), peak, total,...  8.61 us
    all_to_all x1, blocking collectives, body(): lax.all_to_all(mixed_lat, 'lat', split_axis=0, concat_axis=1, tiled=True)  8.41 us
    all_to_all x1, waiting for transfers between devices, body(): lax.all_to_all(key_col, 'lat', split_axis=1, concat_axis=0, tiled=True)  5.37 us
    all_to_all x1, waiting for transfers between devices, body(): lax.all_to_all(value_col, 'lat', split_axis=1, concat_axis=0, tiled=True)  5.31 us
    dynamic_update_slice x8, local copies, waits for them, and re-layouts, body(): lax.map(one_row, (queries, keys, project(piece, value_lon), peak, total,...  5.3 us
    all_to_all x1, waiting for transfers between devices, body(): lax.all_to_all(query_col, 'lat', split_axis=1, concat_axis=0, tiled=True)  4.95 us
    all_to_all x1, starting transfers between devices, body(): lax.all_to_all(key_col, 'lat', split_axis=1, concat_axis=0, tiled=True)  4.72 us
  transfers between devices with their start and end apart: 4, of which 4 were waited for; matrix products, arithmetic and copies ran while one was open for 4% of the time, Pallas kernels for 0%

commit v1 on v0

--- a/solution.py
+++ b/solution.py
@@ -1,8 +1,20 @@
+import functools
 import math
 import jax
 import jax.numpy as jnp
 from jax import lax
 from jax.sharding import PartitionSpec as P
+
+
+def column_draw(q_in, group_axis):
+    arr_out = lax.all_to_all(
+        jnp.stack(jnp.split(q_in, lax.axis_size(group_axis), axis=0)), group_axis, 0, 0
+    )
+    x_now = jnp.concatenate(arr_out, axis=1)
+    return x_now
+
+
+map_notes_over_axis = functools.partial(column_draw, group_axis="lat")
 
 
 def normalize(values, gain):
@@ -116,7 +128,7 @@
         lax.all_to_all(value_col, "lat", split_axis=1, concat_axis=0, tiled=True),
     )
     mixed_lat = attend_lat(query_col, key_col, value_col, temp_lat, bias_lat)
-    returned = lax.all_to_all(mixed_lat, "lat", split_axis=0, concat_axis=1, tiled=True)
+    returned = map_notes_over_axis(mixed_lat)
     second = first + jnp.dot(returned, out_lat, preferred_element_type=jnp.float32)
     normed_mlp = normalize(second, norm_mlp)
     gate = jnp.dot(normed_mlp, w_gate, preferred_element_type=jnp.float32)

time: 113 us -> 114 us (level)
  no operation moved by 1% of the time
where the time goes in v1:
time: 114 us; the launch traced here: 113 us
  waiting for transfers between devices  39.5 us (35%)
  local copies, waits for them, and re-layouts  20.1 us (18%)
  between operations  13.8 us (12%)
  matrix products  11.6 us (10%)
  starting transfers between devices  11.4 us (10%)
  blocking collectives  8.41 us (7%)
  other arithmetic  7.85 us (7%)
    all_gather x1, waiting for transfers between devices, body(): piece = lax.all_gather(normed, 'lon', axis=1, tiled=True)  23.9 us
    dynamic_slice x32, local copies, waits for them, and re-layouts, body(): lax.map(one_row, (queries, keys, project(piece, value_lon), peak, total,...  8.61 us
    all_to_all x1, blocking collectives, column_draw(): lax.all_to_all(jnp.stack(jnp.split(q_in, lax.axis_size(group_axis), axis=...  8.41 us
    all_to_all x1, waiting for transfers between devices, body(): lax.all_to_all(key_col, 'lat', split_axis=1, concat_axis=0, tiled=True)  5.37 us
    dynamic_update_slice x8, local copies, waits for them, and re-layouts, body(): lax.map(one_row, (queries, keys, project(piece, value_lon), peak, total,...  5.31 us
    all_to_all x1, waiting for transfers between devices, body(): lax.all_to_all(value_col, 'lat', split_axis=1, concat_axis=0, tiled=True)  5.31 us
    all_to_all x1, waiting for transfers between devices, body(): lax.all_to_all(query_col, 'lat', split_axis=1, concat_axis=0, tiled=True)  4.95 us
    all_to_all x1, starting transfers between devices, body(): lax.all_to_all(key_col, 'lat', split_axis=1, concat_axis=0, tiled=True)  4.73 us
  transfers between devices with their start and end apart: 4, of which 4 were waited for; matrix products, arithmetic and copies ran while one was open for 4% of the time, Pallas kernels for 0%

profile of v1, /device:TPU:0, one launch (start us, length us, event | category | flops | bytes accessed | tf_op | source)
XLA Modules:
  0.0 113.2 jit_solution(10143421632284966262)
XLA Ops:
  6.6 1.1 fusion.35
  7.7 1.7 %fusion.37 = bf16[8,32,256]{2,1,0:T(8,128)(2,1)} fusion(bf16[8,32,256]{2,1,0:T(8,128)(2,1)} %param.21, f32[256]{0:T(256)} %param.22, f32[8,32]{1,0:T(8,128)S(1)} %add_rsqrt_fusion.2), kind=kLoop, calls=%fused_computation.60 | loop fusion | flops 262144 | bytes 264192 | tf_op jit(solution)/shard_map/convert_element_type | solution.py:22
  9.4 1.2 %convolution_convert_fusion.5 = bf16[8,32,256]{2,1,0:T(8,128)(2,1)S(1)} fusion(bf16[8,32,256]{2,1,0:T(8,128)(2,1)} %fusion.37, bf16[256,256]{1,0:T(8,128)(2,1)} %param.23), kind=kOutput, calls=%fused_computation.36 | convolution fusion | flops 33619968 | bytes 393216 | tf_op jit(solution)/shard_map/dot_general | solution.py:26
  10.6 1.0 reshape.138
  11.7 23.9 %all-gather.2.cloned.1.call-done = bf16[8,256,256]{2,1,0:T(8,128)(2,1)} async-done(((bf16[8,32,256]{2,1,0:T(8,128)(2,1)}), bf16[8,256,256]{2,1,0:T(8,128)(2,1)}) %all-gather.2.cloned.1.call-update) | async-done | bytes 1048592 | tf_op jit(solution)/shard_map/all_gather | solution.py:82
  35.6 1.7 %convolution_convert_fusion.1 = bf16[8,256,256]{2,1,0:T(8,128)(2,1)S(1)} fusion(bf16[8,256,256]{2,1,0:T(8,128)(2,1)} %all-gather.2.cloned.1.call-done, bf16[256,256]{1,0:T(8,128)(2,1)S(1)} %copy-done.3), kind=kOutput, calls=%fused_computation.20 | convolution fusion | flops 268959744 | bytes 2228224 | tf_op jit(solution)/shard_map/dot_general | solution.py:26
  37.4 0.4 convolution_convert_fusion
  38.1 21.5 %while.13 = (s32[]{:T(128)}, f32[8,8,32]{2,1,0:T(8,128)S(1)}, f32[8,32,256]{1,2,0:T(8,128)}, bf16[8,32,8,32]{3,2,1,0:T(8,128)(2,1)}, bf16[8,256,256]{2,1,0:T(8,1...) while((s32[]{:T(128)}, f32[8,8,32]{2,1,0:T(8,128)S(1)}, ...), condition=%wide.region_4.5_spmd.clone, body=%wide.region_1.4_spmd.clone.sunk | while | flops 8946946 | bytes 2429245 | solution.py:115
  38.4 0.9 constant_dynamic-slice_fusion.6
  39.8 0.2 fusion.81
  40.1 0.7 constant_dynamic-update-slice_fusion.2
  41.1 0.9 constant_dynamic-slice_fusion.6
  42.5 0.2 fusion.81
  42.8 0.7 constant_dynamic-update-slice_fusion.2
  43.8 0.9 constant_dynamic-slice_fusion.6
  45.5 0.7 constant_dynamic-update-slice_fusion.2
  46.5 0.9 constant_dynamic-slice_fusion.6
  48.1 0.7 constant_dynamic-update-slice_fusion.2
  49.1 0.9 constant_dynamic-slice_fusion.6
  50.6 0.2 fusion.81
  50.8 0.7 constant_dynamic-update-slice_fusion.2
  51.8 0.9 constant_dynamic-slice_fusion.6
  53.5 0.7 constant_dynamic-update-slice_fusion.2
  54.5 0.9 constant_dynamic-slice_fusion.6
  55.9 0.2 fusion.81
  56.2 0.7 constant_dynamic-update-slice_fusion.2
  57.2 0.9 constant_dynamic-slice_fusion.6
  58.9 0.7 constant_dynamic-update-slice_fusion.2
  59.6 1.4 %fusion.16 = bf16[8,32,256]{1,2,0:T(8,128)(2,1)S(1)} fusion(f32[8,32,256]{1,2,0:T(8,128)} %get-tuple-element.53, f32[8,32,8]{1,2,0:T(8,128)S(1)} %bitcast.137), kind=kLoop, calls=%fused_computation.38 | loop fusion | flops 131072 | bytes 401408 | tf_op jit(solution)/shard_map/convert_element_type | solution.py:119
  61.0 0.4 multiply_reduce_fusion.1
  61.5 0.3 copy-done.5
  62.0 0.7 copy.49
  62.8 4.7 %all-to-all-start.2 = ((bf16[8,32,256]{2,0,1:T(8,128)(2,1)}), bf16[8,32,256]{2,0,1:T(8,128)(2,1)S(1)}, u32[]{:S(2)}, u32[]{:S(2)}) async-start(bf16[8,32,256]{2,0,1:T(8,128)(2,1)} %copy.49), calls=%async_computation.2 | async-start | bytes 262144 | tf_op jit(solution)/shard_map/all_to_all | solution.py:127
  67.7 0.7 copy.47
  68.4 5.4 %all-to-all-done.2 = bf16[8,32,256]{2,0,1:T(8,128)(2,1)S(1)} async-done(((bf16[8,32,256]{2,0,1:T(8,128)(2,1)}), bf16[8,32,256]{2,0,1:T(8,128)(2,1)S(1)}, u32[]{:S(2)}, u32[]{:S(2)}) %all-to-all-start.2) | async-done | bytes 131104 | tf_op jit(solution)/shard_map/all_to_all | solution.py:127
  73.8 3.3 %all-to-all-start.1 = ((bf16[8,32,256]{2,0,1:T(8,128)(2,1)}), bf16[8,32,256]{2,0,1:T(8,128)(2,1)S(1)}, u32[]{:S(2)}, u32[]{:S(2)}) async-start(bf16[8,32,256]{2,0,1:T(8,128)(2,1)} %copy.47), calls=%async_computation.1 | async-start | bytes 262144 | tf_op jit(solution)/shard_map/all_to_all | solution.py:126
  77.3 0.7 copy.45
  78.1 5.0 %all-to-all-done.1 = bf16[8,32,256]{2,0,1:T(8,128)(2,1)S(1)} async-done(((bf16[8,32,256]{2,0,1:T(8,128)(2,1)}), bf16[8,32,256]{2,0,1:T(8,128)(2,1)S(1)}, u32[]{:S(2)}, u32[]{:S(2)}) %all-to-all-start.1) | async-done | bytes 131104 | tf_op jit(solution)/shard_map/all_to_all | solution.py:126
  83.0 3.3 %all-to-all-start = ((bf16[8,32,256]{2,0,1:T(8,128)(2,1)}), bf16[8,32,256]{2,0,1:T(8,128)(2,1)S(1)}, u32[]{:S(2)}, u32[]{:S(2)}) async-start(bf16[8,32,256]{2,0,1:T(8,128)(2,1)} %copy.45), calls=%async_computation | async-start | bytes 262144 | tf_op jit(solution)/shard_map/all_to_all | solution.py:128
  86.9 5.3 %all-to-all-done = bf16[8,32,256]{2,0,1:T(8,128)(2,1)S(1)} async-done(((bf16[8,32,256]{2,0,1:T(8,128)(2,1)}), bf16[8,32,256]{2,0,1:T(8,128)(2,1)S(1)}, u32[]{:S(2)}, u32[]{:S(2)}) %all-to-all-start) | async-done | bytes 131104 | tf_op jit(solution)/shard_map/all_to_all | solution.py:128
  92.5 0.9 fusion.57
  93.4 0.3 fusion.22
  93.7 0.8 fusion.11
  95.2 8.4 %all_to_all.50 = bf16[4,8,8,256]{3,2,1,0:T(8,128)(2,1)S(1)} all-to-all(bf16[4,8,8,256]{3,2,1,0:T(8,128)(2,1)S(1)} %pad_maximum_fusion), channel_id=1, replica_groups=mesh['lon'=8,'lat'=4] {'lat'}, dimensions={0} | all-to-all | bytes 262144 | tf_op jit(solution)/shard_map/all_to_all | solution.py:10
  103.6 0.3 multiply_reduce_fusion
  104.0 0.3 fusion.28
  104.3 0.6 copy-done.14
  105.1 1.2 %fusion.15 = bf16[8,32,256]{2,1,0:T(8,128)(2,1)} fusion(f32[8,32,256]{2,1,0:T(8,128)S(1)} %get-tuple-element.136, f32[8,32,1024]{2,1,0:T(8,128)S(1)} %fusion.28, bf16[1024,256]{1,0:T(8,128)(2,1)S(1)} %copy-done.14, bf16[256,1024]{1,0:T(8,128)(2,1)S(1)} %copy-done.15, f32[256]{0:T(256)S(1)} %copy-done.12, f32[8,32]{1,0:T(8,128)S(1)} %add_rsqrt_fusion), kind=kOutput, calls=%fused_computation.32 | convolution fusion | flops 270336000 | bytes 2492416 | tf_op jit(solution)/shard_map/dot_general | solution.py:137
  (134 shorter events, 10.7 us)
Async XLA Ops:
  6.5 97.4 %copy-start = (bf16[256,1024]{1,0:T(8,128)(2,1)S(1)}, bf16[256,1024]{1,0:T(8,128)(2,1)}, u32[]{:S(2)}) copy-start(bf16[256,1024]{1,0:T(8,128)(2,1)} %param.37) | copy-start | bytes 1572868
  6.5 5.1 %copy-start.16 = (f32[8]{0:T(128)S(1)}, f32[8]{0:T(128)}, u32[]{:S(2)}) copy-start(f32[8]{0:T(128)} %param.27) | copy-start | bytes 100
  6.5 5.1 %copy-start.13 = (f32[8]{0:T(128)S(1)}, f32[8]{0:T(128)}, u32[]{:S(2)}) copy-start(f32[8]{0:T(128)} %param.35) | copy-start | bytes 100
  6.5 29.1 %copy-start.3 = (bf16[256,256]{1,0:T(8,128)(2,1)S(1)}, bf16[256,256]{1,0:T(8,128)(2,1)}, u32[]{:S(2)}) copy-start(bf16[256,256]{1,0:T(8,128)(2,1)} %param.24) | copy-start | bytes 393220
  6.5 29.1 %all-gather.2.cloned.1.call-start = ((), (), s32[]{:S(2)}) async-start(), calls=%async_computation.4 | async-start | bytes 1179648 | tf_op jit(solution)/shard_map/all_gather | solution.py:82
  11.7 25.7 %copy-start.4 = (bf16[256,256]{1,0:T(8,128)(2,1)S(1)}, bf16[256,256]{1,0:T(8,128)(2,1)}, u32[]{:S(2)}) copy-start(bf16[256,256]{1,0:T(8,128)(2,1)} %param.25) | copy-start | bytes 393220
  35.6 1.8 %copy-start.1 = (bf16[8,256,256]{2,1,0:T(8,128)(2,1)S(1)}, bf16[8,256,256]{2,1,0:T(8,128)(2,1)}, u32[]{:S(2)}) copy-start(bf16[8,256,256]{2,1,0:T(8,128)(2,1)} %all-gather.2.cloned.1.call-done) | copy-start | bytes 3145732
  37.4 0.7 copy-start.10
  59.6 1.4 %copy-start.2 = (bf16[8,32,256]{2,1,0:T(8,128)(2,1)S(1)}, bf16[8,32,256]{2,1,0:T(8,128)(2,1)}, u32[]{:S(2)}) copy-start(bf16[8,32,256]{2,1,0:T(8,128)(2,1)} %param.21) | copy-start | bytes 393220
  59.6 1.4 %copy-start.9 = (bf16[256,256]{1,0:T(8,128)(2,1)S(1)}, bf16[256,256]{1,0:T(8,128)(2,1)}, u32[]{:S(2)}) copy-start(bf16[256,256]{1,0:T(8,128)(2,1)} %param.26) | copy-start | bytes 393220
  59.6 1.8 %copy-start.11 = (f32[256]{0:T(256)S(1)}, f32[256]{0:T(256)}, u32[]{:S(2)}) copy-start(f32[256]{0:T(256)} %param.29) | copy-start | bytes 3076
  60.9 0.9 copy-start.5
  61.0 6.6 %copy-start.6 = (bf16[256,256]{1,0:T(8,128)(2,1)S(1)}, bf16[256,256]{1,0:T(8,128)(2,1)}, u32[]{:S(2)}) copy-start(bf16[256,256]{1,0:T(8,128)(2,1)} %param.30) | copy-start | bytes 393220
  61.4 15.7 %copy-start.7 = (bf16[256,256]{1,0:T(8,128)(2,1)S(1)}, bf16[256,256]{1,0:T(8,128)(2,1)}, u32[]{:S(2)}) copy-start(bf16[256,256]{1,0:T(8,128)(2,1)} %param.32) | copy-start | bytes 393220
  62.8 23.6 %copy-start.17 = (f32[8]{0:T(128)S(1)}, f32[8]{0:T(128)}, u32[]{:S(2)}) copy-start(f32[8]{0:T(128)} %param.34) | copy-start | bytes 100
  62.8 11.0 %all-to-all-start.2 = ((bf16[8,32,256]{2,0,1:T(8,128)(2,1)}), bf16[8,32,256]{2,0,1:T(8,128)(2,1)S(1)}, u32[]{:S(2)}, u32[]{:S(2)}) async-start(bf16[8,32,256]{2,0,1:T(8,128)(2,1)} %copy.49), calls=%async_computation.2 | async-start | bytes 262144 | tf_op jit(solution)/shard_map/all_to_all | solution.py:127
  73.8 9.2 %all-to-all-start.1 = ((bf16[8,32,256]{2,0,1:T(8,128)(2,1)}), bf16[8,32,256]{2,0,1:T(8,128)(2,1)S(1)}, u32[]{:S(2)}, u32[]{:S(2)}) async-start(bf16[8,32,256]{2,0,1:T(8,128)(2,1)} %copy.47), calls=%async_computation.1 | async-start | bytes 262144 | tf_op jit(solution)/shard_map/all_to_all | solution.py:126
  83.0 9.2 %all-to-all-start = ((bf16[8,32,256]{2,0,1:T(8,128)(2,1)}), bf16[8,32,256]{2,0,1:T(8,128)(2,1)S(1)}, u32[]{:S(2)}, u32[]{:S(2)}) async-start(bf16[8,32,256]{2,0,1:T(8,128)(2,1)} %copy.45), calls=%async_computation | async-start | bytes 262144 | tf_op jit(solution)/shard_map/all_to_all | solution.py:128
  94.6 9.1 %copy-start.8 = (bf16[256,256]{1,0:T(8,128)(2,1)S(1)}, bf16[256,256]{1,0:T(8,128)(2,1)}, u32[]{:S(2)}) copy-start(bf16[256,256]{1,0:T(8,128)(2,1)} %param.33) | copy-start | bytes 393220
  94.9 9.1 %copy-start.12 = (f32[256]{0:T(256)S(1)}, f32[256]{0:T(256)}, u32[]{:S(2)}) copy-start(f32[256]{0:T(256)} %param.36) | copy-start | bytes 3076
  103.9 1.0 copy-start.14
  103.9 1.2 %copy-start.15 = (bf16[256,1024]{1,0:T(8,128)(2,1)S(1)}, bf16[256,1024]{1,0:T(8,128)(2,1)}, u32[]{:S(2)}) copy-start(bf16[256,1024]{1,0:T(8,128)(2,1)} %param.38) | copy-start | bytes 1572868
Sparse Core Ops, SparseCore 0:
  9.5 26.0 all-gather.1
